TPU v7x, 32 devices: a 4x4x1 block of a 4x4x8 slice. The times are simulated.
32 devices in a mesh: dp: 1 (over z), vp: 32 (over y, x, core).
Axes of the slice: x: 4, y: 4, z: 1, core: 2. Of those that a mesh axis runs over, the one named last changes fastest.
The devices are a block of a 4x4x8 slice.
Arguments:
- hidden: bfloat16 [1024, 5120], P(('dp', 'vp'))
- target: int32 [1024], P('dp')
- norm_gain: bfloat16 [5120], replicated
- head_weight: bfloat16 [5120, 151936], P(None, 'vp')
Outputs:
- output 1: float32 [1024], P('dp')
- output 2: float32 [1024], P('dp')
- output 3: float32 [1], P('dp')
All inputs are finite; a program needn't handle non-finite values.
Results may differ from a plain program's by a relative error of at most 0.001.
Values are sent between devices in bfloat16 or wider.
A program may use at most 768 MiB of HBM per device.

v0:
```python
import jax
import jax.numpy as jnp
from jax import lax
from jax.sharding import PartitionSpec as P

NORM_EPS = 1e-6


def solution(mesh):
    def local_step(hidden, target, norm_gain, head_weight):
        hidden_f32 = hidden.astype(jnp.float32)
        inv_rms = lax.rsqrt(jnp.mean(hidden_f32 * hidden_f32, axis=-1, keepdims=True) + NORM_EPS)
        normed = (hidden_f32 * inv_rms * norm_gain.astype(jnp.float32)).astype(jnp.bfloat16)
        group_rows = lax.all_gather(normed, "vp", axis=0, tiled=True)
        logits = jnp.dot(group_rows, head_weight, preferred_element_type=jnp.float32)
        vocab_local = head_weight.shape[1]
        local_ids = target - lax.axis_index("vp") * vocab_local
        row_max = lax.pmax(jnp.max(logits, axis=-1), "vp")
        shifted = logits - row_max[:, None]
        exp_vals = jnp.exp(shifted)
        col_ids = jnp.arange(vocab_local, dtype=jnp.int32)
        target_shift = jnp.sum(jnp.where(col_ids[None, :] == local_ids[:, None], shifted, 0.0), axis=-1)
        local_stats = jnp.stack([jnp.sum(exp_vals, axis=-1), jnp.sum(exp_vals * shifted, axis=-1), target_shift])
        row_stats = lax.psum(local_stats, "vp")
        log_total = jnp.log(row_stats[0])
        log_prob = row_stats[2] - log_total
        entropy = log_total - row_stats[1] / row_stats[0]
        return log_prob, entropy, jnp.mean(log_prob).reshape(1)

    return jax.shard_map(local_step, mesh=mesh, in_specs=(P(("dp", "vp"), None), P("dp"), P(None), P(None, "vp")), out_specs=(P("dp"), P("dp"), P("dp")), check_vma=False)
```

profile of v0, /device:TPU:97, one launch (start us, length us, event | category | flops | bytes accessed | tf_op | source)
XLA Modules:
  0.0 236.5 jit_solution(10530944410091660962)
XLA Ops:
  7.2 0.1 all-gather.2.cloned.1.call-start
  7.2 0.7 convert_element_type.10
  8.0 1.1 fusion.1
  9.1 1.8 fusion.3
  10.9 0.1 all-gather.2.cloned.1.call-update
  11.0 0.7 broadcast_subtract_fusion
  11.7 56.0 %all-gather.2.cloned.1.call-done = bf16[1024,5120]{1,0:T(8,128)(2,1)} async-done(((bf16[32,5120]{1,0:T(8,128)(2,1)}), bf16[1024,5120]{1,0:T(8,128)(2,1)}) %all-gather.2.cloned.1.call-update) | async-done | bytes 10485776 | tf_op jit(solution)/shard_map/all_gather | solution.py:14
  67.7 59.4 %fusion.6 = (f32[1024]{0:T(1024)S(1)}, f32[1024,4748]{0,1:T(8,128)}) fusion(bf16[1024,5120]{1,0:T(8,128)(2,1)} %all-gather.2.cloned.1.call-done, bf16[5120,4748]{0,1:T(8,128)(2,1)} %param.7), kind=kOutput, calls=%fused_computation.18 | convolution fusion | flops 49791250432 | bytes 78557184 | tf_op jit(solution)/shard_map/dot_general | solution.py:15
  127.1 44.7 %pmax.7 = f32[1024]{0:T(1024)S(1)} all-reduce(f32[1024]{0:T(1024)S(1)} %get-tuple-element.9), channel_id=1, replica_groups=mesh['dp'=1,'vp'=32] {'vp'}, use_global_device_ids=true, to_apply=%region_2.0 | all-reduce | flops 1024 | bytes 8192 | tf_op jit(solution)/shard_map/pmax | solution.py:18
  171.8 10.2 %exponential_reduce_fusion = (f32[1024]{0:T(1024)S(1)}, f32[1024]{0:T(1024)S(1)}, f32[1024]{0:T(1024)S(1)}) fusion(f32[1024,4748]{0,1:T(8,128)} %get-tuple-element.10, f32[1024]{0:T(1024)S(1)} %pmax.7, s32[1024]{0:T(1024)S(1)} %broadcast_subtract_fusion), kind=kLoop, calls=%fused_computation.1 | loop fusion | flops 34030592 | bytes 19468288 | tf_op jit(solution)/shard_map/reduce_sum | solution.py:23
  181.9 44.7 %psum.7 = f32[3,1024]{1,0:T(4,128)S(1)} all-reduce(f32[3,1024]{1,0:T(4,128)S(1)} %pad_maximum_fusion), channel_id=1, replica_groups=mesh['dp'=1,'vp'=32] {'vp'}, use_global_device_ids=true, to_apply=%region_6.7 | all-reduce | flops 3072 | bytes 24576 | tf_op jit(solution)/shard_map/psum | solution.py:24
  226.7 1.2 fusion.5
  (2 shorter events, 0.0 us)
Async XLA Ops:
  7.2 60.5 %all-gather.2.cloned.1.call-start = ((), (), s32[]{:S(2)}) async-start(), calls=%async_computation | async-start | bytes 10813440 | tf_op jit(solution)/shard_map/all_gather | solution.py:14
Sparse Core Ops, SparseCore 0:
  11.1 56.5 all-gather.1
where the time goes:
time: 237 us
  blocking collectives  89.4 us (38%)
  matrix products  59.4 us (25%)
  waiting for transfers between devices  56 us (24%)
  between operations  15.9 us (7%)
  other arithmetic  15.8 us (7%)
    dot_general x1, matrix products, local_step(): jnp.dot(group_rows, head_weight, preferred_element_type=jnp.float32)  59.4 us
    all_gather x1, waiting for transfers between devices, local_step(): group_rows = lax.all_gather(normed, 'vp', axis=0, tiled=True)  56 us
    psum x1, blocking collectives, local_step(): row_stats = lax.psum(local_stats, 'vp')  44.7 us
    pmax x1, blocking collectives, local_step(): row_max = lax.pmax(jnp.max(logits, axis=-1), 'vp')  44.7 us
    reduce_sum x1, other arithmetic, local_step(): jnp.sum(exp_vals, axis=-1)  10.2 us
  transfers between devices with their start and end apart: 1, of which 1 were waited for; matrix products, arithmetic and copies ran while one was open for 0% of the time, Pallas kernels for 0%

commit v1 on v0

v1 whole, which is shorter than its diff:
```python
import functools
import math

import jax
import jax.numpy as jnp
from jax import lax
from jax.experimental import pallas as pl
from jax.experimental.pallas import tpu as pltpu
from jax.sharding import PartitionSpec as P

NORM_EPS = 1e-6
TILE = 256
LANES = 128
STEP = 528
PIECE = 88
SEGMENTS = 3
FLOOR = -200.0


def _chunks(vocab):
    units = -(-vocab // 16)
    count = -(-units * 16 // STEP)
    ends = [units * (i + 1) // count * 16 for i in range(count)]
    return [(start, end - start) for start, end in zip([0] + ends, ends)]


def _kernel(
    side, hid_hbm, tgt_hbm, rest_hbm, w_hbm, lp_ref, ent_ref, mean_ref,
    hid, tgt, w, h, ids, local_ids, ms, zs, ss, ts, stat, hold, recv, zbuf,
    in_sem, w_sem, s_send, s_recv, st_send, st_recv,
):
    n = 2 * side * side
    rows, depth = hid.shape
    vocab = w_hbm.shape[0]
    ktiles = depth // TILE
    group = rows * side
    me = lax.axis_index("vp")
    core = lax.rem(me, 2)
    x = lax.rem(me // 2, side)
    y = me // (2 * side)
    first = jnp.where(core == 0, x, y)
    second = jnp.where(core == 0, y, x)
    partner = me + 1 - 2 * core

    def device(p1, p2):
        return jnp.where(core == 0, (p2 * side + p1) * 2, (p1 * side + p2) * 2 + 1)

    def turn(p, by):
        return lax.rem(p + by + side, side)

    def group_row(kind, p2):
        return (kind * side + p2) * group

    whole = vocab // 16 * 16
    small = [
        pltpu.make_async_copy(src, dst, in_sem.at[i])
        for i, (src, dst) in enumerate(((hid_hbm, hid), (rest_hbm, w.at[pl.ds(whole, 16), :]), (tgt_hbm, tgt)))
    ]
    for c in small:
        c.start()
    chunks = _chunks(vocab)
    per = -(-len(chunks) // SEGMENTS)
    cuts = [chunks[i][0] for i in range(0, len(chunks), per)] + [whole]

    def head_copy(i):
        at = pl.ds(cuts[i], cuts[i + 1] - cuts[i])
        return pltpu.make_async_copy(w_hbm.at[at, :], w.at[at, :], w_sem.at[i])

    for i in range(len(cuts) - 1):
        head_copy(i).start()

    barrier = pltpu.get_barrier_semaphore()

    def greet(k, _):
        pl.semaphore_signal(barrier, inc=1, device_id={"vp": lax.rem(me + k, n)}, device_id_type=pl.DeviceIdType.MESH)
        return 0

    lax.fori_loop(1, n, greet, 0)

    small[0].wait()
    small[1].wait()
    xf = hid[...].astype(jnp.float32)
    inv = lax.rsqrt(jnp.mean(xf * xf, axis=-1, keepdims=True) + NORM_EPS)
    own = pl.multiple_of(group_row(core, second) + first * rows, rows)
    gain = w[whole : whole + 16, :].astype(jnp.float32)[vocab - whole : vocab - whole + 1]
    h[pl.ds(own, rows), :] = (xf * inv * gain).astype(jnp.bfloat16)

    def send(slot, row, count, to):
        at = h.at[pl.ds(pl.multiple_of(row, 16), count), :]
        return pltpu.make_async_remote_copy(
            src_ref=at, dst_ref=at, send_sem=s_send.at[slot], recv_sem=s_recv.at[slot],
            device_id={"vp": to}, device_id_type=pl.DeviceIdType.MESH,
        )

    half = rows // 2
    next1, prev1, far1 = turn(first, 1), turn(first, -1), turn(first, 2)
    next2, prev2, far2 = turn(second, 1), turn(second, -1), turn(second, 2)
    up1, down1 = device(next1, second), device(prev1, second)
    up2, down2 = device(first, next2), device(first, prev2)
    base = group_row(core, second)
    below, above, across = base + prev1 * rows, base + next1 * rows, base + far1 * rows
    pair = 2 * rows
    mine, lower, upper, opposite = (group_row(core, p) for p in (second, prev2, next2, far2))

    pl.semaphore_wait(barrier, n - 1)
    sends = [
        send(0, own, half, up1),
        send(1, own + half, half, down1),
        send(2, own + half, half, up1),
        send(3, own, half, down1),
        send(4, own, rows, partner),
    ]
    for c in sends:
        c.start()
    arrive = lambda slot, count: send(slot, 0, count, partner).wait_recv()

    small[2].wait()
    lane1 = lax.broadcasted_iota(jnp.int32, (1, LANES), 1)
    part = lane1 // rows
    turned = [tgt[...]] + [pltpu.roll(tgt[...], i * rows, 1) for i in range(1, side)]

    def by_part(pieces):
        out = pieces[-1]
        for i in range(len(pieces) - 2, -1, -1):
            out = jnp.where(part == i, pieces[i], out)
        return out

    def cut(arrays, row, move):
        return arrays[move % side][row : row + 1]

    for g in range(side):
        ids[g : g + 1, :] = by_part([cut(turned, 2 * g + i // 2, i - i % 2 * 2) for i in range(side)])
        ids[side + g : side + g + 1, :] = by_part(
            [cut(turned, 2 * i + g // 2, i - g % 2 * 2 - 1) for i in range(side)]
        )

    arrive(0, half)
    sends.append(send(5, below, half, up1))
    sends[-1].start()
    arrive(1, half)
    sends.append(send(6, above + half, half, down1))
    sends[-1].start()
    arrive(2, half)
    arrive(3, half)
    sends += [send(7, below, rows, partner), send(8, above, rows, partner)]
    sends[-2].start()
    sends[-1].start()
    arrive(5, half)
    arrive(6, half)
    sends.append(send(9, across, rows, partner))
    sends[-1].start()
    later = [
        send(10, mine, pair, up2),
        send(11, mine + pair, pair, down2),
        send(12, mine + pair, pair, up2),
        send(13, mine, pair, down2),
    ]
    for c in later:
        c.start()
    sends += later

    forward = [send(14, lower, pair, up2), send(15, upper + pair, pair, down2)]
    share1 = [send(16, lower, pair, partner), send(17, upper + pair, pair, partner)]
    share2 = [send(18, lower + pair, pair, partner), send(19, upper, pair, partner)]
    share3 = [send(20, opposite, pair, partner), send(21, opposite + pair, pair, partner)]
    sends += forward + share1 + share2 + share3

    def pass_on(arrivals, copies):
        for slot in arrivals:
            arrive(slot, pair)
        for c in copies:
            c.start()

    def stat_copy(slot, count, to):
        return pltpu.make_async_remote_copy(
            src_ref=stat.at[pl.ds(slot, count)], dst_ref=recv.at[pl.ds(slot, count), me],
            send_sem=st_send, recv_sem=st_recv,
            device_id={"vp": to}, device_id_type=pl.DeviceIdType.MESH,
        )

    def spread(slot, count):
        def one(k, _):
            stat_copy(slot, count, lax.rem(me + k, n)).start()
            return 0

        lax.fori_loop(1, n, one, 0)

    lane = lax.broadcasted_iota(jnp.int32, (8, LANES), 1)
    sub = lax.broadcasted_iota(jnp.int32, (8, LANES), 0)

    def update(kind, row, tiles, keep=None):
        at = pl.ds(kind * LANES, LANES)
        last = len(tiles) - 1
        if keep is not None:
            tiles[last] = jnp.where(keep, tiles[last], -jnp.inf)
        old = ms[:, at]
        level = list(tiles)
        while len(level) > 1:
            level = [jnp.maximum(*level[i : i + 2]) if i + 1 < len(level) else level[i] for i in range(0, len(level), 2)]
        top = jnp.maximum(old, level[0])
        down = jnp.maximum(old - top, FLOOR)
        scale = jnp.exp(down)
        z, t = zs[:, at], ts[:, at]
        s = scale * (ss[:, at] + z * down)
        z = scale * z
        local = local_ids[kind]
        for i, v in enumerate(tiles):
            d = v - top
            hit = local == row + 8 * i
            if keep is not None and i == last:
                d = jnp.maximum(d, FLOOR)
                hit = jnp.logical_and(hit, keep)
            e = jnp.exp(d)
            z = z + e
            s = s + e * d
            t = jnp.where(hit, v, t)
        ms[:, at], zs[:, at], ss[:, at], ts[:, at] = top, z, s, t

    def reset(lo, hi):
        ms[...] = jnp.full(ms.shape, -jnp.inf, jnp.float32)
        for r in (zs, ss, ts):
            r[...] = jnp.zeros(r.shape, jnp.float32)
        for kind, place in ((0, y), (1, x)):
            a = ids[pl.ds(kind * side + turn(place, lo), 1), :]
            b = ids[pl.ds(kind * side + turn(place, hi), 1), :]
            wanted = jnp.where(lane1 < pair, a, b) - me * vocab
            local_ids[kind] = jnp.broadcast_to(wanted, (8, LANES)) - sub

    def close():
        out = []
        for kind in range(2):
            at = pl.ds(kind * LANES, LANES)
            m, z = ms[:, at], zs[:, at]
            top = jnp.max(m, axis=0, keepdims=True)
            down = jnp.maximum(m - top, FLOOR)
            scale = jnp.exp(down)
            out += [
                top,
                jnp.sum(scale * z, axis=0, keepdims=True),
                jnp.sum(scale * (ss[:, at] + z * down), axis=0, keepdims=True),
                jnp.sum(ts[:, at], axis=0, keepdims=True),
            ]
        return jnp.concatenate(out, axis=0)

    def block_work(accs, b):
        lo = jnp.where(b == 0, 0, jnp.where(b == 1, -1, jnp.where(b == 2, 1, 2)))
        hi = jnp.where(b == 0, 0, jnp.where(b == 1, 1, jnp.where(b == 2, -1, 2)))
        offsets = []
        for kind, place in ((0, y), (1, x)):
            offsets.append(pl.multiple_of(group_row(kind, turn(place, lo)), pair))
            offsets.append(pl.multiple_of(group_row(kind, turn(place, hi)) + pair, pair))

        @pl.when(b == 0)
        def _():
            for slot in (4, 7, 8, 9):
                arrive(slot, rows)

        for j in range(1, 4):

            @pl.when(b == j)
            def _():
                arrive(14 + 2 * j, pair)
                arrive(15 + 2 * j, pair)

        reset(lo, hi)

        def tokens(k):
            return jnp.concatenate([h[pl.ds(o, pair), k * TILE : (k + 1) * TILE] for o in offsets], axis=0)

        def product(c):
            start, count = chunks[c]
            rhs = jnp.concatenate([h[pl.ds(o, pair), :] for o in offsets], axis=0)
            return lax.dot_general(
                w[start : start + count, :], rhs, (((1,), (1,)), ((), ())), preferred_element_type=jnp.float32
            )

        def statistics(c, z):
            start, count = chunks[c]
            for r in range(0, count, PIECE):
                for kind in range(2):
                    tiles = [z[r + j : r + j + 8, kind * LANES : (kind + 1) * LANES] for j in range(0, min(PIECE, count - r), 8)]
                    edge = start + r + 8 * len(tiles)
                    keep = sub < vocab - edge + 8 if edge > vocab else None
                    update(kind, start + r, tiles, keep)

        for c in range(len(chunks)):
            if c % per == 0:

                @pl.when(b == 0)
                def _():
                    head_copy(c // per).wait()

            if c == 2 * per:

                @pl.when(b == 0)
                def _():
                    pass_on((10, 11), forward + share1)

            if c == per:

                @pl.when(b == 1)
                def _():
                    pass_on((12, 13), share2)

                @pl.when(b == 2)
                def _():
                    pass_on((14, 15), share3)

            zbuf[c % 2, : chunks[c][1]] = product(c)
            if c:
                statistics(c - 1, zbuf.at[(c - 1) % 2])
        statistics(len(chunks) - 1, zbuf.at[(len(chunks) - 1) % 2])
        finish(b)

        return 0

    def finish(b):
        p = close()

        def put(slot, v):
            stat[slot] = v
            recv[slot, me] = v

        @pl.when(b == 0)
        def _():
            put(0, p)
            spread(0, 1)

        @pl.when(b == 1)
        def _():
            hold[...] = p

        @pl.when(b == 2)
        def _():
            q = hold[...]
            put(1, jnp.where(lane < pair, q, p))
            put(2, jnp.where(lane < pair, p, q))
            spread(1, 2)

        @pl.when(b == 3)
        def _():
            put(3, p)
            spread(3, 1)

    def one_block(b, _):
        return block_work(None, b)

    lax.fori_loop(0, 4, one_block, 0)

    for c in sends:
        c.wait_send()
    everything = recv.at[:, pl.ds(0, n - 1)]
    pltpu.make_async_copy(everything, everything, st_recv).wait()
    pltpu.make_async_copy(everything, everything, st_send).wait()

    slot_of = {0: 0, side - 1: 1, 1: 2, 2: 3}
    low = sub < 4
    q4 = lax.rem(sub, 4)
    lps, ents = [None] * (2 * side), [None] * (2 * side)
    for g in range(side):

        def value(d):
            dx, dy = (d // 2) % side, d // (2 * side)
            a = recv[slot_of[(g - dy) % side], d]
            b = recv[slot_of[(g - dx) % side], d]
            return jnp.where(low, a, b)

        top = functools.reduce(jnp.maximum, [value(d) for d in range(n)])
        total = jnp.zeros((8, LANES), jnp.float32)
        for d in range(n):
            v = value(d)
            gap = v - top
            down = jnp.where(low, jnp.broadcast_to(gap[0:1, :], (8, LANES)), jnp.broadcast_to(gap[4:5, :], (8, LANES)))
            down = jnp.maximum(down, FLOOR)
            scaled = v * jnp.exp(down)
            moved = pltpu.roll(scaled * down, 1, 0)
            total = total + jnp.where(q4 == 3, v, scaled) + jnp.where(q4 == 2, moved, 0.0)
        for k in range(2):
            m, z, s, t = top[4 * k : 4 * k + 1], *(total[4 * k + i : 4 * k + i + 1] for i in (1, 2, 3))
            log_z = jnp.log(z)
            lps[k * side + g] = (t - m) - log_z
            ents[k * side + g] = log_z - s / z

    for parts, ref in ((lps, lp_ref), (ents, ent_ref)):
        both = jnp.concatenate(parts, axis=0)
        moved = [both] + [pltpu.roll(both, i * rows, 1) for i in range(1, side)]
        for r in range(2 * side):
            q, hx = r // 2, r % 2
            ref[r : r + 1, :] = by_part(
                [
                    cut(moved, q, -2 * hx),
                    cut(moved, side + 2 * hx, 1 - q),
                    cut(moved, q, 1 - 2 * hx),
                    cut(moved, side + 2 * hx + 1, 3 - q),
                ]
            )
    mean_ref[0] = jnp.sum(lp_ref[...]) / (2 * side * group)


def solution(mesh):
    n = mesh.shape["vp"]
    side = math.isqrt(n // 2)

    def local_step(hidden, target, norm_gain, head_weight):
        rows, depth = hidden.shape
        tokens = target.shape[0]
        group = rows * side
        vocab = head_weight.shape[1]
        whole = vocab // 16 * 16
        rest = jnp.concatenate([head_weight.T[whole:], norm_gain[None]])
        rest = jnp.pad(rest, ((0, 16 - rest.shape[0]), (0, 0)))
        lp, entropy, mean = pl.pallas_call(
            functools.partial(_kernel, side),
            out_shape=(
                jax.ShapeDtypeStruct((2 * side, group), jnp.float32),
                jax.ShapeDtypeStruct((2 * side, group), jnp.float32),
                jax.ShapeDtypeStruct((1,), jnp.float32),
            ),
            in_specs=[pl.BlockSpec(memory_space=pl.ANY)] * 4,
            out_specs=(
                pl.BlockSpec(memory_space=pltpu.VMEM),
                pl.BlockSpec(memory_space=pltpu.VMEM),
                pl.BlockSpec(memory_space=pltpu.SMEM),
            ),
            scratch_shapes=[
                pltpu.VMEM((rows, depth), jnp.bfloat16),
                pltpu.VMEM((2 * side, group), jnp.int32),
                pltpu.VMEM((whole + 16, depth), jnp.bfloat16),
                pltpu.VMEM((tokens, depth), jnp.bfloat16),
                pltpu.VMEM((2 * side, group), jnp.int32),
                pltpu.VMEM((2, 8, LANES), jnp.int32),
                *[pltpu.VMEM((8, 2 * LANES), jnp.float32)] * 4,
                pltpu.VMEM((side, 8, LANES), jnp.float32),
                pltpu.VMEM((8, LANES), jnp.float32),
                pltpu.VMEM((side, n, 8, LANES), jnp.float32),
                pltpu.VMEM((2, STEP, TILE), jnp.float32),
                pltpu.SemaphoreType.DMA((3,)),
                pltpu.SemaphoreType.DMA((SEGMENTS,)),
                pltpu.SemaphoreType.DMA((22,)),
                pltpu.SemaphoreType.DMA((22,)),
                pltpu.SemaphoreType.DMA,
                pltpu.SemaphoreType.DMA,
            ],
            compiler_params=pltpu.CompilerParams(
                collective_id=0, has_side_effects=True, vmem_limit_bytes=67043328
            ),
            name="score",
        )(hidden, target.reshape(2 * side, group), rest, head_weight.T)
        return lp.reshape(tokens), entropy.reshape(tokens), mean

    return jax.shard_map(
        local_step,
        mesh=mesh,
        in_specs=(P(("dp", "vp"), None), P("dp"), P(None), P(None, "vp")),
        out_specs=(P("dp"), P("dp"), P("dp")),
        check_vma=False,
    )
```

time: 237 us -> 102 us (0.43)
  Pallas kernels: 0 us -> 94.6 us
  blocking collectives: 89.4 us -> 0 us
  matrix products: 59.4 us -> 0 us
  waiting for transfers between devices: 56 us -> 0 us
  other arithmetic: 15.8 us -> 0.72 us
  between operations: 15.9 us -> 2.41 us
  local copies, waits for them, and re-layouts: 0 us -> 4.19 us
    pallas_call x0 -> x1, Pallas kernels: none -> 94.6 us  [local_step(): pl.pallas_call(functools.partial(_kernel, side), out_shape=(jax.ShapeDtyp...]
    dot_general x1 -> x0, matrix products: 59.4 us -> none  [local_step(): jnp.dot(group_rows, head_weight, preferred_element_type=jnp.float32)]
    all_gather x1 -> x0, waiting for transfers between devices: 56 us -> none  [local_step(): group_rows = lax.all_gather(normed, 'vp', axis=0, tiled=True)]
    psum x1 -> x0, blocking collectives: 44.7 us -> none  [local_step(): row_stats = lax.psum(local_stats, 'vp')]
    pmax x1 -> x0, blocking collectives: 44.7 us -> none  [local_step(): row_max = lax.pmax(jnp.max(logits, axis=-1), 'vp')]
    reduce_sum x3 -> x0, other arithmetic: 12.5 us -> none  [the longest x1 10.2 us: local_step(): jnp.sum(exp_vals, axis=-1)]
    convert_element_type x2 -> x0, other arithmetic: 2.54 us -> none  [the longest x1 1.84 us: local_step(): (hidden_f32 * inv_rms * norm_gain.astype(jnp.float32)).astype(jnp.bfloat16)]
    unnamed x0 -> x2, local copies, waits for them, and re-layouts: none -> 2.54 us
  transfers between devices with their start and end apart: 1 -> 0, of which waited for: 1 -> 0; matrix products, arithmetic and copies ran while one was open for 0% -> 0% of each run, Pallas kernels for 0% -> 0%
where the time goes in v1:
time: 102 us
  Pallas kernels  94.6 us (93%)
  local copies, waits for them, and re-layouts  4.19 us (4%)
  between operations  2.41 us (2%)
    pallas_call x1, Pallas kernels, local_step(): pl.pallas_call(functools.partial(_kernel, side), out_shape=(jax.ShapeDtyp...  94.6 us
    unnamed x2, local copies, waits for them, and re-layouts  2.54 us

profile of v1, /device:TPU:97, one launch (start us, length us, event | category | flops | bytes accessed | tf_op | source)
XLA Modules:
  0.0 101.9 jit_solution(4183513761638436410)
XLA Ops:
  0.6 0.7 broadcast_in_dim.3
  1.3 0.9 slice.4
  2.3 0.7 fusion.2.rest_hbm
  3.0 94.6 %score.1 = (f32[8,128]{1,0:T(8,128)}, f32[8,128]{1,0:T(8,128)}, f32[1]{0:T(128)}) custom-call(bf16[32,5120]{1,0:T(8,128)(2,1)} %hid_hbm.1, s32[8,128]{1,0:T(8,128)} %bitcast.6, bf16[16,5120]{1,0:T(8,128)(2,1)} %fusion.2.rest_hbm, bf16[4748,5120]{1,0:T(8,128)(2,1)} %bitcast.5), custom_call_target="tpu_custom_call" | custom-call | tf_op jit(solution)/shard_map/score/pallas_call | solution.py:412
  97.6 1.3 %copy.10 = f32[1024]{0:T(1024)} copy(f32[1024]{0:T(1024)} %bitcast.8) | data formatting | bytes 8192
  98.9 1.3 %copy.11 = f32[1024]{0:T(1024)} copy(f32[1024]{0:T(1024)} %bitcast.7) | data formatting | bytes 8192

commit v2 on v1

--- a/solution.py
+++ b/solution.py
@@ -11,22 +11,28 @@
 NORM_EPS = 1e-6
 TILE = 256
 LANES = 128
-STEP = 528
-PIECE = 88
+PIECE = 80
 SEGMENTS = 3
+PAIRS = 2
 FLOOR = -200.0
 
 
 def _chunks(vocab):
     units = -(-vocab // 16)
-    count = -(-units * 16 // STEP)
-    ends = [units * (i + 1) // count * 16 for i in range(count)]
-    return [(start, end - start) for start, end in zip([0] + ends, ends)]
+    count = SEGMENTS * PAIRS
+    size = -(-units // (2 * count)) * 2
+    out, start = [], 0
+    for _ in range(count):
+        both = min(size, units - start)
+        for rows in (both - both // 2, both // 2):
+            out.append((start * 16, rows * 16))
+            start += rows
+    return out
 
 
 def _kernel(
-    side, hid_hbm, tgt_hbm, rest_hbm, w_hbm, lp_ref, ent_ref, mean_ref,
-    hid, tgt, w, h, ids, local_ids, ms, zs, ss, ts, stat, hold, recv, zbuf,
+    side, hid_hbm, tgt_hbm, gain_hbm, rest_hbm, w_hbm, parts_ref, mean_ref,
+    hid, tgt, gain, w, h, ids, local_ids, ms, zs, ss, ts, stat, hold, recv, zbuf,
     in_sem, w_sem, s_send, s_recv, st_send, st_recv,
 ):
     n = 2 * side * side
@@ -51,15 +57,29 @@
     def group_row(kind, p2):
         return (kind * side + p2) * group
 
+    half = rows // 2
+    next1, prev1, far1 = turn(first, 1), turn(first, -1), turn(first, 2)
+    next2, prev2, far2 = turn(second, 1), turn(second, -1), turn(second, 2)
+    up1, down1 = device(next1, second), device(prev1, second)
+    up2, down2 = device(first, next2), device(first, prev2)
+
+    near = (partner, up1, down1, up2, down2)
+    barrier = pltpu.get_barrier_semaphore()
+    for to in near:
+        pl.semaphore_signal(barrier, inc=1, device_id={"vp": to}, device_id_type=pl.DeviceIdType.MESH)
+
     whole = vocab // 16 * 16
+    twice = 16 - vocab % 16
     small = [
         pltpu.make_async_copy(src, dst, in_sem.at[i])
-        for i, (src, dst) in enumerate(((hid_hbm, hid), (rest_hbm, w.at[pl.ds(whole, 16), :]), (tgt_hbm, tgt)))
+        for i, (src, dst) in enumerate(
+            ((hid_hbm, hid), (gain_hbm, gain), (tgt_hbm, tgt), (rest_hbm, w.at[pl.ds(whole, 16), :]))
+        )
     ]
     for c in small:
         c.start()
     chunks = _chunks(vocab)
-    per = -(-len(chunks) // SEGMENTS)
+    per = 2 * PAIRS
     cuts = [chunks[i][0] for i in range(0, len(chunks), per)] + [whole]
 
     def head_copy(i):
@@ -67,23 +87,17 @@
         return pltpu.make_async_copy(w_hbm.at[at, :], w.at[at, :], w_sem.at[i])
 
     for i in range(len(cuts) - 1):
-        head_copy(i).start()
-
-    barrier = pltpu.get_barrier_semaphore()
-
-    def greet(k, _):
-        pl.semaphore_signal(barrier, inc=1, device_id={"vp": lax.rem(me + k, n)}, device_id_type=pl.DeviceIdType.MESH)
-        return 0
-
-    lax.fori_loop(1, n, greet, 0)
+        head_copy(i).start(priority=1)
 
     small[0].wait()
     small[1].wait()
     xf = hid[...].astype(jnp.float32)
     inv = lax.rsqrt(jnp.mean(xf * xf, axis=-1, keepdims=True) + NORM_EPS)
     own = pl.multiple_of(group_row(core, second) + first * rows, rows)
-    gain = w[whole : whole + 16, :].astype(jnp.float32)[vocab - whole : vocab - whole + 1]
-    h[pl.ds(own, rows), :] = (xf * inv * gain).astype(jnp.bfloat16)
+    for i in range(depth // LANES):
+        cols = slice(i * LANES, (i + 1) * LANES)
+        part = xf[:, cols] * inv * gain[i : i + 1, :].astype(jnp.float32)
+        h[pl.ds(own, rows), cols] = part.astype(jnp.bfloat16)
 
     def send(slot, row, count, to):
         at = h.at[pl.ds(pl.multiple_of(row, 16), count), :]
@@ -92,17 +106,12 @@
             device_id={"vp": to}, device_id_type=pl.DeviceIdType.MESH,
         )
 
-    half = rows // 2
-    next1, prev1, far1 = turn(first, 1), turn(first, -1), turn(first, 2)
-    next2, prev2, far2 = turn(second, 1), turn(second, -1), turn(second, 2)
-    up1, down1 = device(next1, second), device(prev1, second)
-    up2, down2 = device(first, next2), device(first, prev2)
     base = group_row(core, second)
     below, above, across = base + prev1 * rows, base + next1 * rows, base + far1 * rows
     pair = 2 * rows
     mine, lower, upper, opposite = (group_row(core, p) for p in (second, prev2, next2, far2))
 
-    pl.semaphore_wait(barrier, n - 1)
+    pl.semaphore_wait(barrier, len(near))
     sends = [
         send(0, own, half, up1),
         send(1, own + half, half, down1),
@@ -179,22 +188,16 @@
         )
 
     def spread(slot, count):
-        def one(k, _):
+        for k in range(1, n):
             stat_copy(slot, count, lax.rem(me + k, n)).start()
-            return 0
-
-        lax.fori_loop(1, n, one, 0)
 
     lane = lax.broadcasted_iota(jnp.int32, (8, LANES), 1)
     sub = lax.broadcasted_iota(jnp.int32, (8, LANES), 0)
 
-    def update(kind, row, tiles, keep=None):
+    def update(kind, tiles):
         at = pl.ds(kind * LANES, LANES)
-        last = len(tiles) - 1
-        if keep is not None:
-            tiles[last] = jnp.where(keep, tiles[last], -jnp.inf)
         old = ms[:, at]
-        level = list(tiles)
+        level = [v if keep is None else jnp.where(keep, v, -jnp.inf) for _, keep, v in tiles]
         while len(level) > 1:
             level = [jnp.maximum(*level[i : i + 2]) if i + 1 < len(level) else level[i] for i in range(0, len(level), 2)]
         top = jnp.maximum(old, level[0])
@@ -204,11 +207,11 @@
         s = scale * (ss[:, at] + z * down)
         z = scale * z
         local = local_ids[kind]
-        for i, v in enumerate(tiles):
+        for row, keep, v in tiles:
             d = v - top
-            hit = local == row + 8 * i
-            if keep is not None and i == last:
-                d = jnp.maximum(d, FLOOR)
+            hit = local == row
+            if keep is not None:
+                d = jnp.where(keep, d, FLOOR)
                 hit = jnp.logical_and(hit, keep)
             e = jnp.exp(d)
             z = z + e
@@ -261,6 +264,8 @@
             def _():
                 arrive(14 + 2 * j, pair)
                 arrive(15 + 2 * j, pair)
+                if j == 3:
+                    spread(0, 3)
 
         reset(lo, hi)
 
@@ -278,10 +283,14 @@
             start, count = chunks[c]
             for r in range(0, count, PIECE):
                 for kind in range(2):
-                    tiles = [z[r + j : r + j + 8, kind * LANES : (kind + 1) * LANES] for j in range(0, min(PIECE, count - r), 8)]
-                    edge = start + r + 8 * len(tiles)
-                    keep = sub < vocab - edge + 8 if edge > vocab else None
-                    update(kind, start + r, tiles, keep)
+                    tiles = []
+                    for j in range(r, min(r + PIECE, count), 8):
+                        row, keep = start + j, None
+                        if row >= whole:
+                            keep = sub >= twice - (row - whole)
+                            row -= twice
+                        tiles.append((row, keep, z[j : j + 8, kind * LANES : (kind + 1) * LANES]))
+                    update(kind, tiles)
 
         for c in range(len(chunks)):
             if c % per == 0:
@@ -289,6 +298,8 @@
                 @pl.when(b == 0)
                 def _():
                     head_copy(c // per).wait()
+                    if c == 2 * per:
+                        small[3].wait()
 
             if c == 2 * per:
 
@@ -324,7 +335,6 @@
         @pl.when(b == 0)
         def _():
             put(0, p)
-            spread(0, 1)
 
         @pl.when(b == 1)
         def _():
@@ -335,7 +345,6 @@
             q = hold[...]
             put(1, jnp.where(lane < pair, q, p))
             put(2, jnp.where(lane < pair, p, q))
-            spread(1, 2)
 
         @pl.when(b == 3)
         def _():
@@ -356,7 +365,7 @@
     slot_of = {0: 0, side - 1: 1, 1: 2, 2: 3}
     low = sub < 4
     q4 = lax.rem(sub, 4)
-    lps, ents = [None] * (2 * side), [None] * (2 * side)
+    logs, shifts, ratios = ([None] * (2 * side) for _ in range(3))
     for g in range(side):
 
         def value(d):
@@ -377,16 +386,16 @@
             total = total + jnp.where(q4 == 3, v, scaled) + jnp.where(q4 == 2, moved, 0.0)
         for k in range(2):
             m, z, s, t = top[4 * k : 4 * k + 1], *(total[4 * k + i : 4 * k + i + 1] for i in (1, 2, 3))
-            log_z = jnp.log(z)
-            lps[k * side + g] = (t - m) - log_z
-            ents[k * side + g] = log_z - s / z
-
-    for parts, ref in ((lps, lp_ref), (ents, ent_ref)):
+            logs[k * side + g] = jnp.log(z)
+            shifts[k * side + g] = t - m
+            ratios[k * side + g] = s / z
+
+    for i, parts in enumerate((shifts, logs, ratios)):
         both = jnp.concatenate(parts, axis=0)
         moved = [both] + [pltpu.roll(both, i * rows, 1) for i in range(1, side)]
         for r in range(2 * side):
             q, hx = r // 2, r % 2
-            ref[r : r + 1, :] = by_part(
+            parts_ref[i, r : r + 1, :] = by_part(
                 [
                     cut(moved, q, -2 * hx),
                     cut(moved, side + 2 * hx, 1 - q),
@@ -394,7 +403,7 @@
                     cut(moved, side + 2 * hx + 1, 3 - q),
                 ]
             )
-    mean_ref[0] = jnp.sum(lp_ref[...]) / (2 * side * group)
+    mean_ref[0] = jnp.sum(parts_ref[0] - parts_ref[1]) / (2 * side * group)
 
 
 def solution(mesh):
@@ -407,24 +416,22 @@
         group = rows * side
         vocab = head_weight.shape[1]
         whole = vocab // 16 * 16
-        rest = jnp.concatenate([head_weight.T[whole:], norm_gain[None]])
-        rest = jnp.pad(rest, ((0, 16 - rest.shape[0]), (0, 0)))
-        lp, entropy, mean = pl.pallas_call(
+        rest = head_weight.T[vocab - 16 :]
+        parts, mean = pl.pallas_call(
             functools.partial(_kernel, side),
             out_shape=(
-                jax.ShapeDtypeStruct((2 * side, group), jnp.float32),
-                jax.ShapeDtypeStruct((2 * side, group), jnp.float32),
+                jax.ShapeDtypeStruct((3, 2 * side, group), jnp.float32),
                 jax.ShapeDtypeStruct((1,), jnp.float32),
             ),
-            in_specs=[pl.BlockSpec(memory_space=pl.ANY)] * 4,
+            in_specs=[pl.BlockSpec(memory_space=pl.ANY)] * 5,
             out_specs=(
-                pl.BlockSpec(memory_space=pltpu.VMEM),
                 pl.BlockSpec(memory_space=pltpu.VMEM),
                 pl.BlockSpec(memory_space=pltpu.SMEM),
             ),
             scratch_shapes=[
                 pltpu.VMEM((rows, depth), jnp.bfloat16),
                 pltpu.VMEM((2 * side, group), jnp.int32),
+                pltpu.VMEM((depth // LANES, LANES), jnp.bfloat16),
                 pltpu.VMEM((whole + 16, depth), jnp.bfloat16),
                 pltpu.VMEM((tokens, depth), jnp.bfloat16),
                 pltpu.VMEM((2 * side, group), jnp.int32),
@@ -433,8 +440,8 @@
                 pltpu.VMEM((side, 8, LANES), jnp.float32),
                 pltpu.VMEM((8, LANES), jnp.float32),
                 pltpu.VMEM((side, n, 8, LANES), jnp.float32),
-                pltpu.VMEM((2, STEP, TILE), jnp.float32),
-                pltpu.SemaphoreType.DMA((3,)),
+                pltpu.VMEM((2, _chunks(vocab)[0][1], TILE), jnp.float32),
+                pltpu.SemaphoreType.DMA((4,)),
                 pltpu.SemaphoreType.DMA((SEGMENTS,)),
                 pltpu.SemaphoreType.DMA((22,)),
                 pltpu.SemaphoreType.DMA((22,)),
@@ -445,8 +452,9 @@
                 collective_id=0, has_side_effects=True, vmem_limit_bytes=67043328
             ),
             name="score",
-        )(hidden, target.reshape(2 * side, group), rest, head_weight.T)
-        return lp.reshape(tokens), entropy.reshape(tokens), mean
+        )(hidden, target.reshape(2 * side, group), norm_gain.reshape(depth // LANES, LANES), rest, head_weight.T)
+        shift, log_total, ratio = parts.reshape(3, tokens)
+        return shift - log_total, log_total - ratio, mean
 
     return jax.shard_map(
         local_step,

time: 102 us -> 84.8 us (0.83)
  Pallas kernels: 94.6 us -> 79.3 us
  local copies, waits for them, and re-layouts: 4.19 us -> 1.64 us
    pallas_call x1, Pallas kernels: 94.6 us -> 79.3 us  [local_step(): pl.pallas_call(functools.partial(_kernel, side), out_shape=(jax.ShapeDtyp...]
    unnamed x2 -> x0, local copies, waits for them, and re-layouts: 2.54 us -> none
    sub x0 -> x1, other arithmetic: none -> 1.28 us  [local_step(): return (shift - log_total, log_total - ratio, mean)]
where the time goes in v2:
time: 84.8 us; the launch traced here: 84.6 us
  Pallas kernels  79.3 us (94%)
  between operations  2.4 us (3%)
  local copies, waits for them, and re-layouts  1.64 us (2%)
  other arithmetic  1.28 us (2%)
    pallas_call x1, Pallas kernels, local_step(): pl.pallas_call(functools.partial(_kernel, side), out_shape=(jax.ShapeDtyp...  79.3 us

profile of v2, /device:TPU:97, one launch (start us, length us, event | category | flops | bytes accessed | tf_op | source)
XLA Modules:
  0.0 84.6 jit_solution(15399386667134292796)
XLA Ops:
  0.6 1.6 %slice.7.rest_hbm = bf16[16,5120]{1,0:T(8,128)(2,1)} slice(bf16[4748,5120]{1,0:T(8,128)(2,1)} %bitcast.7), slice={[4732:4748], [0:5120]} | slice | bytes 327680 | tf_op jit(solution)/shard_map/slice | solution.py:419
  2.3 79.3 %score.1 = (f32[3,8,128]{2,1,0:T(8,128)}, f32[1]{0:T(128)}) custom-call(bf16[32,5120]{1,0:T(8,128)(2,1)} %hid_hbm.1, s32[8,128]{1,0:T(8,128)} %bitcast.10, bf16[40,128]{1,0:T(8,128)(2,1)} %bitcast.9, bf16[16,5120]{1,0:T(8,128)(2,1)} %slice.7.rest_hbm, bf16[4748,5120]{1,0:T(8,128)(2,1)} %bitcast.8), custom_call_target="tpu_custom_call" | custom-call | tf_op jit(solution)/shard_map/score/pallas_call | solution.py:420
  81.6 1.3 %subtract_bitcast_fusion = (f32[1024]{0:T(1024)}, f32[1024]{0:T(1024)}) fusion(f32[3,8,128]{2,1,0:T(8,128)} %get-tuple-element.5), kind=kLoop, calls=%fused_computation | loop fusion | flops 2048 | bytes 20480 | tf_op jit(solution)/shard_map/sub | solution.py:457

commit v3 on v2

--- a/solution.py
+++ b/solution.py
@@ -25,18 +25,18 @@
     for _ in range(count):
         both = min(size, units - start)
         for rows in (both - both // 2, both // 2):
-            out.append((start * 16, rows * 16))
+            out.append((start * 16, min(rows * 16, vocab - start * 16)))
             start += rows
     return out
 
 
 def _kernel(
-    side, hid_hbm, tgt_hbm, gain_hbm, rest_hbm, w_hbm, parts_ref, mean_ref,
-    hid, tgt, gain, w, h, ids, local_ids, ms, zs, ss, ts, stat, hold, recv, zbuf,
+    side, hid_hbm, tgt_hbm, gain_hbm, w_hbm, parts_ref, mean_ref,
+    tgt, gain, w, h, ids, local_ids, ms, zs, ss, ts, stat, hold, recv, zbuf, early,
     in_sem, w_sem, s_send, s_recv, st_send, st_recv,
 ):
     n = 2 * side * side
-    rows, depth = hid.shape
+    rows, depth = hid_hbm.shape
     vocab = w_hbm.shape[0]
     ktiles = depth // TILE
     group = rows * side
@@ -68,39 +68,40 @@
     for to in near:
         pl.semaphore_signal(barrier, inc=1, device_id={"vp": to}, device_id_type=pl.DeviceIdType.MESH)
 
-    whole = vocab // 16 * 16
-    twice = 16 - vocab % 16
+    own = pl.multiple_of(group_row(core, second) + first * rows, rows)
+
     small = [
         pltpu.make_async_copy(src, dst, in_sem.at[i])
-        for i, (src, dst) in enumerate(
-            ((hid_hbm, hid), (gain_hbm, gain), (tgt_hbm, tgt), (rest_hbm, w.at[pl.ds(whole, 16), :]))
-        )
+        for i, (src, dst) in enumerate(((hid_hbm, h.at[pl.ds(own, rows), :]), (gain_hbm, gain), (tgt_hbm, tgt)))
     ]
     for c in small:
         c.start()
     chunks = _chunks(vocab)
     per = 2 * PAIRS
-    cuts = [chunks[i][0] for i in range(0, len(chunks), per)] + [whole]
 
     def head_copy(i):
-        at = pl.ds(cuts[i], cuts[i + 1] - cuts[i])
-        return pltpu.make_async_copy(w_hbm.at[at, :], w.at[at, :], w_sem.at[i])
-
-    for i in range(len(cuts) - 1):
+        cols = pl.ds(i * depth // 2, depth // 2)
+        return pltpu.make_async_copy(w_hbm.at[:, cols], w.at[:, cols], w_sem.at[i])
+
+    for i in range(2):
         head_copy(i).start(priority=1)
 
     small[0].wait()
     small[1].wait()
-    xf = hid[...].astype(jnp.float32)
+    xf = h[pl.ds(own, rows), :].astype(jnp.float32)
     inv = lax.rsqrt(jnp.mean(xf * xf, axis=-1, keepdims=True) + NORM_EPS)
-    own = pl.multiple_of(group_row(core, second) + first * rows, rows)
     for i in range(depth // LANES):
         cols = slice(i * LANES, (i + 1) * LANES)
         part = xf[:, cols] * inv * gain[i : i + 1, :].astype(jnp.float32)
         h[pl.ds(own, rows), cols] = part.astype(jnp.bfloat16)
 
-    def send(slot, row, count, to):
-        at = h.at[pl.ds(pl.multiple_of(row, 16), count), :]
+    def view(row, count, part):
+        cols = pl.ds(0, depth) if part is None else pl.ds(part * depth // 2, depth // 2)
+        return h.at[pl.ds(pl.multiple_of(row, 16), count), cols]
+
+    def send(slot, row, count, to, part=None):
+        at = view(row, count, part)
+        slot += 0 if part != 1 else 22
         return pltpu.make_async_remote_copy(
             src_ref=at, dst_ref=at, send_sem=s_send.at[slot], recv_sem=s_recv.at[slot],
             device_id={"vp": to}, device_id_type=pl.DeviceIdType.MESH,
@@ -112,16 +113,25 @@
     mine, lower, upper, opposite = (group_row(core, p) for p in (second, prev2, next2, far2))
 
     pl.semaphore_wait(barrier, len(near))
-    sends = [
-        send(0, own, half, up1),
-        send(1, own + half, half, down1),
-        send(2, own + half, half, up1),
-        send(3, own, half, down1),
-        send(4, own, rows, partner),
-    ]
-    for c in sends:
-        c.start()
-    arrive = lambda slot, count: send(slot, 0, count, partner).wait_recv()
+    sends = []
+
+    def start(*copies):
+        for c in copies:
+            c.start()
+        sends.extend(copies)
+
+    def arrive(slot, count, part=None):
+        send(slot, 0, count, partner, part).wait_recv()
+
+    start(
+        send(0, own, half, up1, 0),
+        send(1, own + half, half, down1, 0),
+        send(2, own + half, half, up1, 0),
+        send(3, own, half, down1, 0),
+        send(4, own, rows, partner, 0),
+        send(0, own, half, up1, 1),
+        send(1, own + half, half, down1, 1),
+    )
 
     small[2].wait()
     lane1 = lax.broadcasted_iota(jnp.int32, (1, LANES), 1)
@@ -143,40 +153,46 @@
             [cut(turned, 2 * i + g // 2, i - g % 2 * 2 - 1) for i in range(side)]
         )
 
-    arrive(0, half)
-    sends.append(send(5, below, half, up1))
-    sends[-1].start()
-    arrive(1, half)
-    sends.append(send(6, above + half, half, down1))
-    sends[-1].start()
-    arrive(2, half)
-    arrive(3, half)
-    sends += [send(7, below, rows, partner), send(8, above, rows, partner)]
-    sends[-2].start()
-    sends[-1].start()
-    arrive(5, half)
-    arrive(6, half)
-    sends.append(send(9, across, rows, partner))
-    sends[-1].start()
-    later = [
-        send(10, mine, pair, up2),
-        send(11, mine + pair, pair, down2),
-        send(12, mine + pair, pair, up2),
-        send(13, mine, pair, down2),
+    arrive(0, half, 0)
+    start(send(5, below, half, up1, 0))
+    arrive(1, half, 0)
+    start(send(6, above + half, half, down1, 0))
+    start(send(2, own + half, half, up1, 1), send(3, own, half, down1, 1), send(4, own, rows, partner, 1))
+    arrive(2, half, 0)
+    arrive(3, half, 0)
+    start(send(7, below, rows, partner, 0), send(8, above, rows, partner, 0))
+    arrive(0, half, 1)
+    start(send(5, below, half, up1, 1))
+    arrive(1, half, 1)
+    start(send(6, above + half, half, down1, 1))
+    arrive(5, half, 0)
+    arrive(6, half, 0)
+    start(send(9, across, rows, partner, 0))
+    arrive(2, half, 1)
+    arrive(3, half, 1)
+    start(send(7, below, rows, partner, 1), send(8, above, rows, partner, 1))
+    quarter_up = jnp.where(first < 2, first, 3 - first)
+    quarter_down = jnp.where(first < 2, 3 - first, first)
+    start(
+        send(10, mine + quarter_up * rows, rows, up2),
+        send(11, mine + quarter_down * rows, rows, down2),
+    )
+    quarters = [
+        send(9, across, rows, partner, 1),
+        send(32, mine + (1 - quarter_up) * rows, rows, up2),
+        send(33, mine + (5 - quarter_down) * rows, rows, down2),
     ]
-    for c in later:
-        c.start()
-    sends += later
+    later = [send(12, mine + pair, pair, up2), send(13, mine, pair, down2)]
 
     forward = [send(14, lower, pair, up2), send(15, upper + pair, pair, down2)]
     share1 = [send(16, lower, pair, partner), send(17, upper + pair, pair, partner)]
     share2 = [send(18, lower + pair, pair, partner), send(19, upper, pair, partner)]
     share3 = [send(20, opposite, pair, partner), send(21, opposite + pair, pair, partner)]
-    sends += forward + share1 + share2 + share3
-
-    def pass_on(arrivals, copies):
+    sends += quarters + later + forward + share1 + share2 + share3
+
+    def pass_on(arrivals, copies, count=pair):
         for slot in arrivals:
-            arrive(slot, pair)
+            arrive(slot, count)
         for c in copies:
             c.start()
 
@@ -188,36 +204,37 @@
         )
 
     def spread(slot, count):
-        for k in range(1, n):
-            stat_copy(slot, count, lax.rem(me + k, n)).start()
+        away = [(min(dy, side - dy) + min(dx, side - dx), dy, dx, dc) for dy in range(side) for dx in range(side) for dc in range(2)]
+        for _, dy, dx, dc in sorted(away, reverse=True)[:-1]:
+            to = (turn(y, dy) * side + turn(x, dx)) * 2 + (core if dc == 0 else 1 - core)
+            stat_copy(slot, count, to).start()
 
     lane = lax.broadcasted_iota(jnp.int32, (8, LANES), 1)
     sub = lax.broadcasted_iota(jnp.int32, (8, LANES), 0)
 
-    def update(kind, tiles):
+    def update(kind, row, v):
         at = pl.ds(kind * LANES, LANES)
+        edge = row + v.shape[0] > vocab
+        v = v.reshape(v.shape[0] // 8, 8, LANES)
+        rows_at = row + 8 * lax.broadcasted_iota(jnp.int32, v.shape, 0)
+        hit = local_ids[kind][None] == rows_at
+        if edge:
+            keep = rows_at + lax.broadcasted_iota(jnp.int32, v.shape, 1) < vocab
+            v = jnp.where(keep, v, -jnp.inf)
+            hit = jnp.logical_and(hit, keep)
         old = ms[:, at]
-        level = [v if keep is None else jnp.where(keep, v, -jnp.inf) for _, keep, v in tiles]
-        while len(level) > 1:
-            level = [jnp.maximum(*level[i : i + 2]) if i + 1 < len(level) else level[i] for i in range(0, len(level), 2)]
-        top = jnp.maximum(old, level[0])
+        top = jnp.maximum(old, jnp.max(v, axis=0))
         down = jnp.maximum(old - top, FLOOR)
         scale = jnp.exp(down)
-        z, t = zs[:, at], ts[:, at]
-        s = scale * (ss[:, at] + z * down)
-        z = scale * z
-        local = local_ids[kind]
-        for row, keep, v in tiles:
-            d = v - top
-            hit = local == row
-            if keep is not None:
-                d = jnp.where(keep, d, FLOOR)
-                hit = jnp.logical_and(hit, keep)
-            e = jnp.exp(d)
-            z = z + e
-            s = s + e * d
-            t = jnp.where(hit, v, t)
-        ms[:, at], zs[:, at], ss[:, at], ts[:, at] = top, z, s, t
+        d = v - top[None]
+        if edge:
+            d = jnp.maximum(d, FLOOR)
+        e = jnp.exp(d)
+        z = zs[:, at]
+        ss[:, at] = scale * (ss[:, at] + z * down) + jnp.sum(e * d, axis=0)
+        zs[:, at] = scale * z + jnp.sum(e, axis=0)
+        ts[:, at] += jnp.sum(jnp.where(hit, v, 0.0), axis=0)
+        ms[:, at] = top
 
     def reset(lo, hi):
         ms[...] = jnp.full(ms.shape, -jnp.inf, jnp.float32)
@@ -245,20 +262,20 @@
             ]
         return jnp.concatenate(out, axis=0)
 
-    def block_work(accs, b):
-        lo = jnp.where(b == 0, 0, jnp.where(b == 1, -1, jnp.where(b == 2, 1, 2)))
-        hi = jnp.where(b == 0, 0, jnp.where(b == 1, 1, jnp.where(b == 2, -1, 2)))
+    def block_work(b):
+        if isinstance(b, int):
+            lo = hi = 0
+        else:
+            lo = jnp.where(b == 1, -1, jnp.where(b == 2, 1, 2))
+            hi = jnp.where(b == 1, 1, jnp.where(b == 2, -1, 2))
         offsets = []
         for kind, place in ((0, y), (1, x)):
             offsets.append(pl.multiple_of(group_row(kind, turn(place, lo)), pair))
             offsets.append(pl.multiple_of(group_row(kind, turn(place, hi)) + pair, pair))
 
-        @pl.when(b == 0)
-        def _():
-            for slot in (4, 7, 8, 9):
-                arrive(slot, rows)
-
         for j in range(1, 4):
+            if isinstance(b, int):
+                break
 
             @pl.when(b == j)
             def _():
@@ -269,57 +286,65 @@
 
         reset(lo, hi)
 
-        def tokens(k):
-            return jnp.concatenate([h[pl.ds(o, pair), k * TILE : (k + 1) * TILE] for o in offsets], axis=0)
-
-        def product(c):
-            start, count = chunks[c]
-            rhs = jnp.concatenate([h[pl.ds(o, pair), :] for o in offsets], axis=0)
+        def product(c, part=None):
+            first_row, count = chunks[c]
+            cols = slice(0, depth) if part is None else slice(part * depth // 2, (part + 1) * depth // 2)
+            rhs = jnp.concatenate([h[pl.ds(o, pair), cols] for o in offsets], axis=0)
             return lax.dot_general(
-                w[start : start + count, :], rhs, (((1,), (1,)), ((), ())), preferred_element_type=jnp.float32
+                w[first_row : first_row + count, cols], rhs, (((1,), (1,)), ((), ())),
+                preferred_element_type=jnp.float32,
             )
 
         def statistics(c, z):
             start, count = chunks[c]
             for r in range(0, count, PIECE):
                 for kind in range(2):
-                    tiles = []
-                    for j in range(r, min(r + PIECE, count), 8):
-                        row, keep = start + j, None
-                        if row >= whole:
-                            keep = sub >= twice - (row - whole)
-                            row -= twice
-                        tiles.append((row, keep, z[j : j + 8, kind * LANES : (kind + 1) * LANES]))
-                    update(kind, tiles)
-
-        for c in range(len(chunks)):
-            if c % per == 0:
-
-                @pl.when(b == 0)
-                def _():
-                    head_copy(c // per).wait()
-                    if c == 2 * per:
-                        small[3].wait()
-
-            if c == 2 * per:
-
-                @pl.when(b == 0)
-                def _():
-                    pass_on((10, 11), forward + share1)
-
-            if c == per:
-
-                @pl.when(b == 1)
-                def _():
-                    pass_on((12, 13), share2)
-
-                @pl.when(b == 2)
-                def _():
-                    pass_on((14, 15), share3)
-
-            zbuf[c % 2, : chunks[c][1]] = product(c)
+                    last = min(r + PIECE, -(-count // 8) * 8)
+                    update(kind, start + r, z[r:last, kind * LANES : (kind + 1) * LANES])
+
+        def run(c, partial=None):
+            if partial is None:
+                zbuf[c % 2, : chunks[c][1]] = product(c)
+            else:
+                zbuf[c % 2, : chunks[c][1]] = partial[c, : chunks[c][1]] + product(c, 1)
             if c:
                 statistics(c - 1, zbuf.at[(c - 1) % 2])
+
+        if isinstance(b, int):
+            head_copy(0).wait()
+            for slot in (4, 7, 8, 9):
+                arrive(slot, rows, 0)
+            for c in range(per):
+                early[c, : chunks[c][1]] = product(c, 0)
+            arrive(5, half, 1)
+            arrive(6, half, 1)
+            for d in quarters:
+                d.start()
+            for c in range(per, len(chunks)):
+                early[c, : chunks[c][1]] = product(c, 0)
+            for slot in (4, 7, 8, 9):
+                arrive(slot, rows, 1)
+            for d in later:
+                d.start()
+            head_copy(1).wait()
+            for c in range(2 * per):
+                run(c, early)
+            pass_on((10, 11, 32, 33), forward + share1, rows)
+            for c in range(2 * per, len(chunks)):
+                run(c, early)
+        else:
+            for c in range(len(chunks)):
+                if c == len(chunks) // 2:
+
+                    @pl.when(b == 1)
+                    def _():
+                        pass_on((12, 13), share2)
+
+                    @pl.when(b == 2)
+                    def _():
+                        pass_on((14, 15), share3)
+
+                run(c)
         statistics(len(chunks) - 1, zbuf.at[(len(chunks) - 1) % 2])
         finish(b)
 
@@ -332,9 +357,9 @@
             stat[slot] = v
             recv[slot, me] = v
 
-        @pl.when(b == 0)
-        def _():
+        if isinstance(b, int):
             put(0, p)
+            return
 
         @pl.when(b == 1)
         def _():
@@ -352,9 +377,10 @@
             spread(3, 1)
 
     def one_block(b, _):
-        return block_work(None, b)
-
-    lax.fori_loop(0, 4, one_block, 0)
+        return block_work(b)
+
+    block_work(0)
+    lax.fori_loop(1, 4, one_block, 0)
 
     for c in sends:
         c.wait_send()
@@ -415,24 +441,21 @@
         tokens = target.shape[0]
         group = rows * side
         vocab = head_weight.shape[1]
-        whole = vocab // 16 * 16
-        rest = head_weight.T[vocab - 16 :]
         parts, mean = pl.pallas_call(
             functools.partial(_kernel, side),
             out_shape=(
                 jax.ShapeDtypeStruct((3, 2 * side, group), jnp.float32),
                 jax.ShapeDtypeStruct((1,), jnp.float32),
             ),
-            in_specs=[pl.BlockSpec(memory_space=pl.ANY)] * 5,
+            in_specs=[pl.BlockSpec(memory_space=pl.ANY)] * 4,
             out_specs=(
                 pl.BlockSpec(memory_space=pltpu.VMEM),
                 pl.BlockSpec(memory_space=pltpu.SMEM),
             ),
             scratch_shapes=[
-                pltpu.VMEM((rows, depth), jnp.bfloat16),
                 pltpu.VMEM((2 * side, group), jnp.int32),
                 pltpu.VMEM((depth // LANES, LANES), jnp.bfloat16),
-                pltpu.VMEM((whole + 16, depth), jnp.bfloat16),
+                pltpu.VMEM((vocab, depth), jnp.bfloat16),
                 pltpu.VMEM((tokens, depth), jnp.bfloat16),
                 pltpu.VMEM((2 * side, group), jnp.int32),
                 pltpu.VMEM((2, 8, LANES), jnp.int32),
@@ -441,10 +464,11 @@
                 pltpu.VMEM((8, LANES), jnp.float32),
                 pltpu.VMEM((side, n, 8, LANES), jnp.float32),
                 pltpu.VMEM((2, _chunks(vocab)[0][1], TILE), jnp.float32),
-                pltpu.SemaphoreType.DMA((4,)),
-                pltpu.SemaphoreType.DMA((SEGMENTS,)),
-                pltpu.SemaphoreType.DMA((22,)),
-                pltpu.SemaphoreType.DMA((22,)),
+                pltpu.VMEM((len(_chunks(vocab)), _chunks(vocab)[0][1], TILE), jnp.float32),
+                pltpu.SemaphoreType.DMA((3,)),
+                pltpu.SemaphoreType.DMA((2,)),
+                pltpu.SemaphoreType.DMA((34,)),
+                pltpu.SemaphoreType.DMA((34,)),
                 pltpu.SemaphoreType.DMA,
                 pltpu.SemaphoreType.DMA,
             ],
@@ -452,7 +476,7 @@
                 collective_id=0, has_side_effects=True, vmem_limit_bytes=67043328
             ),
             name="score",
-        )(hidden, target.reshape(2 * side, group), norm_gain.reshape(depth // LANES, LANES), rest, head_weight.T)
+        )(hidden, target.reshape(2 * side, group), norm_gain.reshape(depth // LANES, LANES), head_weight.T)
         shift, log_total, ratio = parts.reshape(3, tokens)
         return shift - log_total, log_total - ratio, mean
 

time: 84.8 us -> 81.9 us (0.966)
  local copies, waits for them, and re-layouts: 1.64 us -> 0 us
  Pallas kernels: 79.3 us -> 78 us
    slice x1 -> x0, local copies, waits for them, and re-layouts: 1.64 us -> none  [local_step(): rest = head_weight.T[vocab - 16:]]
    pallas_call x1, Pallas kernels: 79.3 us -> 78 us  [local_step(): pl.pallas_call(functools.partial(_kernel, side), out_shape=(jax.ShapeDtyp...]
where the time goes in v3:
time: 81.9 us; the launch traced here: 81.7 us
  Pallas kernels  78 us (95%)
  between operations  2.4 us (3%)
  other arithmetic  1.29 us (2%)
    pallas_call x1, Pallas kernels, local_step(): pl.pallas_call(functools.partial(_kernel, side), out_shape=(jax.ShapeDtyp...  78 us

profile of v3, /device:TPU:97, one launch (start us, length us, event | category | flops | bytes accessed | tf_op | source)
XLA Modules:
  0.0 81.7 jit_solution(555553214499594508)
XLA Ops:
  0.6 78.0 %score.1 = (f32[3,8,128]{2,1,0:T(8,128)}, f32[1]{0:T(128)}) custom-call(bf16[32,5120]{1,0:T(8,128)(2,1)} %hid_hbm.1, s32[8,128]{1,0:T(8,128)} %bitcast.9, bf16[40,128]{1,0:T(8,128)(2,1)} %bitcast.8, bf16[4748,5120]{1,0:T(8,128)(2,1)} %bitcast.7), custom_call_target="tpu_custom_call" | custom-call | tf_op jit(solution)/shard_map/score/pallas_call | solution.py:444
  78.6 1.3 %subtract_bitcast_fusion = (f32[1024]{0:T(1024)}, f32[1024]{0:T(1024)}) fusion(f32[3,8,128]{2,1,0:T(8,128)} %get-tuple-element.5), kind=kLoop, calls=%fused_computation | loop fusion | flops 2048 | bytes 20480 | tf_op jit(solution)/shard_map/sub | solution.py:481
